TPU v7x, 32 devices: a whole 2x2x4 slice. The times are simulated.
32 devices in a mesh: grp: 2 (over core), ex: 16 (over z, y, x).
Axes of the slice: x: 2, y: 2, z: 4, core: 2. Of those that a mesh axis runs over, the one named last changes fastest.
Arguments:
- tokens: bfloat16 [8192, 1024], P(('grp', 'ex')), may hold values from -6 to 6
- expert_ids: int32 [8192], P(('grp', 'ex')), may hold values from 0 to 15, as said below
- slot_ids: int32 [8192], P(('grp', 'ex')), may hold values from 0 to 31, as said below
- centroids: bfloat16 [16, 1024], replicated, may hold values from -0.1875 to 0.1875
- w_in: bfloat16 [16, 1024, 4096], P('ex', None, 'grp'), may hold values from -0.1875 to 0.1875
- w_out: bfloat16 [16, 4096, 1024], P('ex', 'grp'), may hold values from -0.09375 to 0.09375
Outputs:
- combined: bfloat16 [8192, 1024], P(('grp', 'ex'))
Inputs may be any that keep to these rules, and one draw needn't show every extreme that they name: `expert_ids`: within each device's 256 rows, at most 32 rows name one expert; in every device some expert is named by exactly 32 rows, and in each group of 16 devices along ex one expert is named by 32 rows on every device of the group. `slot_ids`: rows of one device that name the same expert have distinct slots.
All inputs are finite; a program needn't handle non-finite values.
Results may differ from a plain program's by a relative error of at most 0.0035.
Values may be sent and summed in bfloat16 or wider, within the bound.
No kernel may reach another device: no remote copies, remote signals or barrier semaphores. Data moves between devices by JAX's collectives and lax.ppermute only.
A program may use at most 128 MiB of HBM per device.

v0:
```python
import jax
import jax.numpy as jnp
from jax import lax
from jax.sharding import PartitionSpec as P


def on_device(tokens, expert_ids, slot_ids, centroids, w_in, w_out):
    experts = centroids.shape[0]
    count_rows = tokens.shape[0]
    model_width = tokens.shape[1]
    capacity = 2 * count_rows // experts
    buffer_rows = expert_ids * capacity + slot_ids
    outgoing = (
        jnp.zeros((experts * capacity, model_width), jnp.bfloat16).at[buffer_rows].set(tokens)
    )
    outgoing = outgoing.reshape(experts, capacity, model_width)
    scores = jnp.dot(tokens, centroids.T, preferred_element_type=jnp.float32)
    columns = jnp.arange(experts, dtype=jnp.int32)
    chosen = jnp.sum(jnp.where(columns[None, :] == expert_ids[:, None], scores, 0.0), axis=1)
    gating = jax.nn.sigmoid(chosen)
    full_in, full_out = (
        lax.all_gather(w_in, "grp", axis=2, tiled=True),
        lax.all_gather(w_out, "grp", axis=1, tiled=True),
    )
    received = lax.all_to_all(outgoing, "ex", split_axis=0, concat_axis=0, tiled=True)
    flat_rows = received.reshape(-1, model_width)
    hidden = jnp.maximum(
        jnp.dot(flat_rows, full_in[0], preferred_element_type=jnp.float32), 0.0
    ).astype(jnp.bfloat16)
    result = jnp.dot(hidden, full_out[0], preferred_element_type=jnp.float32)
    returned = lax.all_to_all(
        result.astype(jnp.bfloat16).reshape(received.shape),
        "ex",
        split_axis=0,
        concat_axis=0,
        tiled=True,
    )
    arrived = returned.reshape(-1, model_width)[buffer_rows]
    mixed_rows = tokens.astype(jnp.float32) + gating[:, None] * arrived.astype(jnp.float32)
    return mixed_rows.astype(jnp.bfloat16)


def solution(mesh):
    in_specs = (
        P(("grp", "ex"), None),
        P(("grp", "ex")),
        P(("grp", "ex")),
        P(),
        P("ex", None, "grp"),
        P("ex", "grp", None),
    )
    out_specs = P(("grp", "ex"), None)
    return jax.shard_map(
        on_device, mesh=mesh, in_specs=in_specs, out_specs=out_specs, check_vma=False
    )
```

profile of v0, /device:TPU:8, one launch (start us, length us, event | category | flops | bytes accessed | tf_op | source)
XLA Modules:
  0.0 110.2 jit_solution(7864859476668906878)
XLA Ops:
  6.5 0.0 copy-start
  6.5 0.0 copy-start.2
  6.5 0.0 copy-start.3
  6.5 0.0 copy-start.1
  6.5 0.0 all-gather.3.cloned.1.call-start
  6.6 0.7 all-gather.3.cloned.1.call-update
  7.3 0.0 all-gather.5.cloned.1.call-start
  7.3 0.7 all-gather.5.cloned.1.call-update
  8.0 0.0 copy-done.2
  8.0 0.0 copy-done.3
  8.1 0.0 copy-done.1
  8.1 1.9 %scatter_custom_fusion = bf16[512,1024]{1,0:T(8,128)(2,1)S(1)} fusion(s32[256]{0:T(256)S(1)} %compare_select_fusion, bf16[256,1024]{1,0:T(8,128)(2,1)S(1)} %copy-done.1, bf16[]{:T(256)} %constant.1.clone.1), kind=kCustom, calls=%fused_computation.12 | custom fusion | bytes 1048578 | tf_op jit(solution)/shard_map/scatter | solution.py:14
  10.0 32.7 %all_to_all.10 = bf16[16,32,1024]{2,1,0:T(8,128)(2,1)S(1)} all-to-all(bf16[16,32,1024]{2,1,0:T(8,128)(2,1)S(1)} %bitcast.22), channel_id=1, replica_groups=mesh['grp'=2,'ex'=16] {'ex'}, dimensions={0} | all-to-all | bytes 2097152 | tf_op jit(solution)/shard_map/all_to_all | solution.py:25
  42.7 0.0 all-gather.3.cloned.1.call-done
  42.7 10.1 %all-gather.5.cloned.1.call-done = bf16[1,4096,1024]{2,1,0:T(8,128)(2,1)} async-done(((bf16[1,2048,1024]{2,1,0:T(8,128)(2,1)}), bf16[1,4096,1024]{2,1,0:T(8,128)(2,1)}) %all-gather.5.cloned.1.call-update) | async-done | bytes 8388624 | tf_op jit(solution)/shard_map/all_gather | solution.py:23
  52.8 15.6 %fusion.9 = bf16[512,1024]{1,0:T(8,128)(2,1)} fusion(bf16[1,4096,1024]{2,1,0:T(8,128)(2,1)} %all-gather.5.cloned.1.call-done, bf16[512,1024]{1,0:T(8,128)(2,1)S(1)} %bitcast.23, bf16[1,1024,4096]{2,1,0:T(8,128)(2,1)} %all-gather.3.cloned.1.call-done), kind=kOutput, calls=%fused_computation.8 | convolution fusion | flops 8594653184 | bytes 18874368 | tf_op jit(solution)/shard_map/dot_general | solution.py:30
  68.4 7.0 %all-to-all-start.1 = ((bf16[16,32,1024]{2,1,0:T(8,128)(2,1)}), bf16[16,32,1024]{2,1,0:T(8,128)(2,1)S(1)}, u32[]{:S(2)}, u32[]{:S(2)}) async-start(bf16[16,32,1024]{2,1,0:T(8,128)(2,1)} %bitcast.4), calls=%async_computation.1 | async-start | bytes 2097152 | tf_op jit(solution)/shard_map/all_to_all | solution.py:31
  75.3 0.0 copy-done
  75.4 0.3 fusion.14
  75.6 25.6 %all-to-all-done.1 = bf16[16,32,1024]{2,1,0:T(8,128)(2,1)S(1)} async-done(((bf16[16,32,1024]{2,1,0:T(8,128)(2,1)}), bf16[16,32,1024]{2,1,0:T(8,128)(2,1)S(1)}, u32[]{:S(2)}, u32[]{:S(2)}) %all-to-all-start.1) | async-done | bytes 1048608 | tf_op jit(solution)/shard_map/all_to_all | solution.py:31
  101.2 1.2 %gather_fusion = bf16[256,1024]{1,0:T(8,128)(2,1)S(1)} fusion(bf16[512,1024]{1,0:T(8,128)(2,1)S(1)} %bitcast.21, s32[1024]{0:T(1024)S(1)} %pad_clamp_fusion), kind=kCustom, calls=%fused_computation | custom fusion | bytes 1049600 | tf_op jit(solution)/shard_map/gather | solution.py:38
  102.4 1.0 add_convert_fusion
  (3 shorter events, 0.0 us)
Async XLA Ops:
  6.5 68.8 %copy-start = (bf16[16,1024]{1,0:T(8,128)(2,1)S(1)}, bf16[16,1024]{1,0:T(8,128)(2,1)}, u32[]{:S(2)}) copy-start(bf16[16,1024]{1,0:T(8,128)(2,1)} %param.9) | copy-start | bytes 98308
  6.5 1.5 %copy-start.2 = (s32[256]{0:T(256)S(1)}, s32[256]{0:T(256)}, u32[]{:S(2)}) copy-start(s32[256]{0:T(256)} %param.7) | copy-start | bytes 3076
  6.5 1.5 %copy-start.3 = (s32[256]{0:T(256)S(1)}, s32[256]{0:T(256)}, u32[]{:S(2)}) copy-start(s32[256]{0:T(256)} %param.8) | copy-start | bytes 3076
  6.5 1.5 %copy-start.1 = (bf16[256,1024]{1,0:T(8,128)(2,1)S(1)}, bf16[256,1024]{1,0:T(8,128)(2,1)}, u32[]{:S(2)}) copy-start(bf16[256,1024]{1,0:T(8,128)(2,1)} %param.6) | copy-start | bytes 1572868
  6.5 36.2 %all-gather.3.cloned.1.call-start = ((), (), s32[]{:S(2)}) async-start(), calls=%async_computation.2 | async-start | bytes 12582912 | tf_op jit(solution)/shard_map/all_gather | solution.py:22
  7.3 45.5 %all-gather.5.cloned.1.call-start = ((), (), s32[]{:S(2)}) async-start(), calls=%async_computation.3 | async-start | bytes 12582912 | tf_op jit(solution)/shard_map/all_gather | solution.py:23
  68.4 32.8 %all-to-all-start.1 = ((bf16[16,32,1024]{2,1,0:T(8,128)(2,1)}), bf16[16,32,1024]{2,1,0:T(8,128)(2,1)S(1)}, u32[]{:S(2)}, u32[]{:S(2)}) async-start(bf16[16,32,1024]{2,1,0:T(8,128)(2,1)} %bitcast.4), calls=%async_computation.1 | async-start | bytes 2097152 | tf_op jit(solution)/shard_map/all_to_all | solution.py:31
Sparse Core Ops, SparseCore 0:
  8.9 21.2 all-gather.2
  31.7 21.0 all-gather.4
where the time goes:
time: 110 us
  waiting for transfers between devices  37 us (34%)
  blocking collectives  32.7 us (30%)
  matrix products  15.8 us (14%)
  between operations  13.5 us (12%)
  starting transfers between devices  7.04 us (6%)
  local copies, waits for them, and re-layouts  3.09 us (3%)
    all_to_all x1, blocking collectives, on_device(): lax.all_to_all(outgoing, 'ex', split_axis=0, concat_axis=0, tiled=True)  32.7 us
    all_to_all x1, waiting for transfers between devices, on_device(): lax.all_to_all(result.astype(jnp.bfloat16).reshape(received.shape), 'ex',...  25.6 us
    dot_general x1, matrix products, on_device(): result = jnp.dot(hidden, full_out[0], preferred_element_type=jnp.float32)  15.6 us
    all_gather x1, waiting for transfers between devices, on_device(): lax.all_gather(w_out, 'grp', axis=1, tiled=True)  10.1 us
    all_to_all x1, starting transfers between devices, on_device(): lax.all_to_all(result.astype(jnp.bfloat16).reshape(received.shape), 'ex',...  6.97 us
  transfers between devices with their start and end apart: 3, of which 2 were waited for; matrix products, arithmetic and copies ran while one was open for 2% of the time, Pallas kernels for 0%

commit v1 on v0

--- a/solution.py
+++ b/solution.py
@@ -9,6 +9,10 @@
     count_rows = tokens.shape[0]
     model_width = tokens.shape[1]
     capacity = 2 * count_rows // experts
+    pair = lax.axis_size("grp")
+    swap = [(i, (i + 1) % pair) for i in range(pair)]
+    far_in = lax.ppermute(w_in, "grp", swap)
+    far_out = lax.ppermute(w_out, "grp", swap)
     buffer_rows = expert_ids * capacity + slot_ids
     outgoing = (
         jnp.zeros((experts * capacity, model_width), jnp.bfloat16).at[buffer_rows].set(tokens)
@@ -18,16 +22,16 @@
     columns = jnp.arange(experts, dtype=jnp.int32)
     chosen = jnp.sum(jnp.where(columns[None, :] == expert_ids[:, None], scores, 0.0), axis=1)
     gating = jax.nn.sigmoid(chosen)
-    full_in, full_out = (
-        lax.all_gather(w_in, "grp", axis=2, tiled=True),
-        lax.all_gather(w_out, "grp", axis=1, tiled=True),
-    )
     received = lax.all_to_all(outgoing, "ex", split_axis=0, concat_axis=0, tiled=True)
     flat_rows = received.reshape(-1, model_width)
-    hidden = jnp.maximum(
-        jnp.dot(flat_rows, full_in[0], preferred_element_type=jnp.float32), 0.0
-    ).astype(jnp.bfloat16)
-    result = jnp.dot(hidden, full_out[0], preferred_element_type=jnp.float32)
+
+    def half(first, second):
+        hidden = jnp.maximum(
+            jnp.dot(flat_rows, first, preferred_element_type=jnp.float32), 0.0
+        ).astype(jnp.bfloat16)
+        return jnp.dot(hidden, second, preferred_element_type=jnp.float32)
+
+    result = half(w_in[0], w_out[0]) + half(far_in[0], far_out[0])
     returned = lax.all_to_all(
         result.astype(jnp.bfloat16).reshape(received.shape),
         "ex",

time: 110 us -> 87.4 us (0.79)
  between operations: 13.5 us -> 0.07 us
  waiting for transfers between devices: 37 us -> 24.5 us
  matrix products: 15.8 us -> 19.2 us
  starting transfers between devices: 7.04 us -> 5.07 us
    all_gather x2 -> x0, waiting for transfers between devices: 10.1 us -> none  [the longest x1 10.1 us: on_device(): lax.all_gather(w_out, 'grp', axis=1, tiled=True)]
    dot_general x1 -> x2, matrix products: 15.6 us -> 18.9 us  [half(): return jnp.dot(hidden, second, preferred_element_type=jnp.float32)]
    all_to_all x1, starting transfers between devices: 6.97 us -> 4.56 us  [on_device(): lax.all_to_all(result.astype(jnp.bfloat16).reshape(received.shape), 'ex',...]
    unnamed x2 -> x0, waiting for transfers between devices: 1.38 us -> none
  transfers between devices with their start and end apart: 3 -> 3, of which waited for: 2 -> 1; matrix products, arithmetic and copies ran while one was open for 2% -> 15% of each run, Pallas kernels for 0% -> 0%
where the time goes in v1:
time: 87.4 us; the launch traced here: 87.1 us
  blocking collectives  33 us (38%)
  waiting for transfers between devices  24.5 us (28%)
  matrix products  19.2 us (22%)
  starting transfers between devices  5.07 us (6%)
  local copies, waits for them, and re-layouts  3.59 us (4%)
  other arithmetic  1.73 us (2%)
    all_to_all x1, blocking collectives, on_device(): lax.all_to_all(outgoing, 'ex', split_axis=0, concat_axis=0, tiled=True)  33 us
    all_to_all x1, waiting for transfers between devices, on_device(): lax.all_to_all(result.astype(jnp.bfloat16).reshape(received.shape), 'ex',...  24.5 us
    dot_general x2, matrix products, half(): return jnp.dot(hidden, second, preferred_element_type=jnp.float32)  18.9 us
    all_to_all x1, starting transfers between devices, on_device(): lax.all_to_all(result.astype(jnp.bfloat16).reshape(received.shape), 'ex',...  4.56 us
    scatter x1, local copies, waits for them, and re-layouts, on_device(): jnp.zeros((experts * capacity, model_width), jnp.bfloat16).at[buffer_rows]  2.41 us
  transfers between devices with their start and end apart: 3, of which 1 were waited for; matrix products, arithmetic and copies ran while one was open for 15% of the time, Pallas kernels for 0%

profile of v1, /device:TPU:8, one launch (start us, length us, event | category | flops | bytes accessed | tf_op | source)
XLA Modules:
  0.0 87.1 jit_solution(12627887598469483533)
XLA Ops:
  0.0 0.0 copy-start
  0.0 0.0 collective-permute-start
  0.0 0.5 collective-permute-start.1
  0.5 0.7 compare_select_fusion
  1.2 2.4 %scatter_custom_fusion = bf16[512,1024]{1,0:T(8,128)(2,1)S(1)} fusion(s32[256]{0:T(256)S(1)} %compare_select_fusion, bf16[256,1024]{1,0:T(8,128)(2,1)} %param.6, bf16[]{:T(256)} %constant.1.clone.1), kind=kCustom, calls=%fused_computation.16 | custom fusion | bytes 1049088 | tf_op jit(solution)/shard_map/scatter | solution.py:18
  3.6 33.0 %all_to_all.10 = bf16[16,32,1024]{2,1,0:T(8,128)(2,1)S(1)} all-to-all(bf16[16,32,1024]{2,1,0:T(8,128)(2,1)S(1)} %bitcast.31), channel_id=1, replica_groups=mesh['grp'=2,'ex'=16] {'ex'}, dimensions={0} | all-to-all | bytes 2097152 | tf_op jit(solution)/shard_map/all_to_all | solution.py:25
  36.6 9.3 %fusion.4 = f32[512,1024]{1,0:T(8,128)} fusion(bf16[1,2048,1024]{2,1,0:T(8,128)(2,1)} %param.11, bf16[512,1024]{1,0:T(8,128)(2,1)S(1)} %bitcast.32, bf16[1,1024,2048]{2,1,0:T(8,128)(2,1)} %param.10), kind=kOutput, calls=%fused_computation.6 | convolution fusion | flops 4297064448 | bytes 11534336 | tf_op jit(solution)/shard_map/dot_general | solution.py:32
  45.9 0.0 copy-start.1
  45.9 0.0 copy-start.2
  45.9 0.0 collective-permute-done
  46.0 0.0 collective-permute-done.1
  46.0 9.6 %add_convert_fusion = bf16[512,1024]{1,0:T(8,128)(2,1)} fusion(f32[512,1024]{1,0:T(8,128)} %fusion.4, bf16[1,2048,1024]{2,1,0:T(8,128)(2,1)} %collective-permute-done.1, bf16[512,1024]{1,0:T(8,128)(2,1)S(1)} %bitcast.33, bf16[1,1024,2048]{2,1,0:T(8,128)(2,1)} %collective-permute-done), kind=kOutput, calls=%fused_computation.12 | convolution fusion | flops 4298113024 | bytes 12582912 | tf_op jit(solution)/shard_map/dot_general | solution.py:32
  55.5 4.6 %all-to-all-start.1 = ((bf16[16,32,1024]{2,1,0:T(8,128)(2,1)}), bf16[16,32,1024]{2,1,0:T(8,128)(2,1)S(1)}, u32[]{:S(2)}, u32[]{:S(2)}) async-start(bf16[16,32,1024]{2,1,0:T(8,128)(2,1)} %bitcast.6), calls=%async_computation.1 | async-start | bytes 2097152 | tf_op jit(solution)/shard_map/all_to_all | solution.py:35
  60.1 0.0 copy-done
  60.1 0.0 copy-done.1
  60.1 0.0 copy-done.2
  60.2 0.3 fusion.14
  60.4 24.5 %all-to-all-done.1 = bf16[16,32,1024]{2,1,0:T(8,128)(2,1)S(1)} async-done(((bf16[16,32,1024]{2,1,0:T(8,128)(2,1)}), bf16[16,32,1024]{2,1,0:T(8,128)(2,1)S(1)}, u32[]{:S(2)}, u32[]{:S(2)}) %all-to-all-start.1) | async-done | bytes 1048608 | tf_op jit(solution)/shard_map/all_to_all | solution.py:35
  84.9 1.2 %gather_fusion = bf16[256,1024]{1,0:T(8,128)(2,1)S(1)} fusion(bf16[512,1024]{1,0:T(8,128)(2,1)S(1)} %bitcast.30, s32[1024]{0:T(1024)S(1)} %pad_clamp_fusion), kind=kCustom, calls=%fused_computation | custom fusion | bytes 1049600 | tf_op jit(solution)/shard_map/gather | solution.py:42
  86.1 1.0 %add_convert_fusion.1 = bf16[256,1024]{1,0:T(8,128)(2,1)} fusion(bf16[256,1024]{1,0:T(8,128)(2,1)S(1)} %gather_fusion, bf16[256,1024]{1,0:T(8,128)(2,1)S(1)} %copy-done.1, f32[256]{0:T(256)S(1)} %add_divide_fusion), kind=kLoop, calls=%fused_computation.15 | loop fusion | flops 1310720 | bytes 1573888 | tf_op jit(solution)/shard_map/convert_element_type | solution.py:44
  (2 shorter events, 0.0 us)
Async XLA Ops:
  0.0 60.1 %copy-start = (bf16[16,1024]{1,0:T(8,128)(2,1)S(1)}, bf16[16,1024]{1,0:T(8,128)(2,1)}, u32[]{:S(2)}) copy-start(bf16[16,1024]{1,0:T(8,128)(2,1)} %param.9) | copy-start | bytes 98308
  0.0 45.9 %collective-permute-start = (bf16[1,1024,2048]{2,1,0:T(8,128)(2,1)}, bf16[1,1024,2048]{2,1,0:T(8,128)(2,1)}, u32[]{:S(2)}, u32[]{:S(2)}) collective-permute-start(bf16[1,1024,2048]{2,1,0:T(8,128)(2,1)} %param.10), channel_id=1, source_target_pairs={{0,16},{16,0},{1,17},{17,1},{2,18},{18,2},{3,19},{19,3},{4,20},{20... | collective-permute-start | bytes 12582920 | tf_op jit(solution)/shard_map/ppermute | solution.py:14
  0.0 45.9 %collective-permute-start.1 = (bf16[1,2048,1024]{2,1,0:T(8,128)(2,1)}, bf16[1,2048,1024]{2,1,0:T(8,128)(2,1)}, u32[]{:S(2)}, u32[]{:S(2)}) collective-permute-start(bf16[1,2048,1024]{2,1,0:T(8,128)(2,1)} %param.11), channel_id=1, source_target_pairs={{0,16},{16,0},{1,17},{17,1},{2,18},{18,2},{3,19},{19,3},{4,20},{20... | collective-permute-start | bytes 12582920 | tf_op jit(solution)/shard_map/ppermute | solution.py:15
  45.9 14.2 %copy-start.1 = (bf16[256,1024]{1,0:T(8,128)(2,1)S(1)}, bf16[256,1024]{1,0:T(8,128)(2,1)}, u32[]{:S(2)}) copy-start(bf16[256,1024]{1,0:T(8,128)(2,1)} %param.6) | copy-start | bytes 1572868
  45.9 14.2 %copy-start.2 = (s32[256]{0:T(256)S(1)}, s32[256]{0:T(256)}, u32[]{:S(2)}) copy-start(s32[256]{0:T(256)} %param.7) | copy-start | bytes 3076
  55.5 29.4 %all-to-all-start.1 = ((bf16[16,32,1024]{2,1,0:T(8,128)(2,1)}), bf16[16,32,1024]{2,1,0:T(8,128)(2,1)S(1)}, u32[]{:S(2)}, u32[]{:S(2)}) async-start(bf16[16,32,1024]{2,1,0:T(8,128)(2,1)} %bitcast.6), calls=%async_computation.1 | async-start | bytes 2097152 | tf_op jit(solution)/shard_map/all_to_all | solution.py:35

commit v2 on v1

v2 whole, which is shorter than its diff:
```python
import functools

import jax
import jax.numpy as jnp
from jax import lax
from jax.experimental import pallas as pl
from jax.experimental.pallas import tpu as pltpu
from jax.sharding import PartitionSpec as P

MIB = 1024 * 1024
COVER = 30_000_000_000


def picks(experts_ref, slots_ref, total_rows, capacity):
    wanted = experts_ref[...] * capacity + slots_ref[...]
    rows = lax.broadcasted_iota(jnp.int32, (total_rows, wanted.shape[1]), 0)
    return jnp.where(rows == wanted, 1.0, 0.0).astype(jnp.bfloat16)


def place_kernel(experts_ref, slots_ref, tokens_ref, out_ref, *, capacity):
    pick = picks(experts_ref, slots_ref, out_ref.shape[0], capacity)
    out_ref[...] = jnp.dot(
        pick, tokens_ref[...], preferred_element_type=jnp.float32
    ).astype(jnp.bfloat16)


def place(expert_ids, slot_ids, tokens, total_rows, capacity):
    return pl.pallas_call(
        functools.partial(place_kernel, capacity=capacity),
        out_shape=jax.ShapeDtypeStruct((total_rows, tokens.shape[1]), jnp.bfloat16),
        compiler_params=pltpu.CompilerParams(vmem_limit_bytes=8 * MIB),
        cost_estimate=pl.CostEstimate(flops=COVER, bytes_accessed=0, transcendentals=0),
        name="place",
    )(expert_ids[None, :], slot_ids[None, :], tokens)


def ffn_kernel(rows_ref, in_a, in_b, out_a, out_b, result_ref):
    def half(rows, first, second):
        hidden = jnp.maximum(
            jnp.dot(rows, first[0], preferred_element_type=jnp.float32), 0.0
        ).astype(jnp.bfloat16)
        return jnp.dot(hidden, second[0], preferred_element_type=jnp.float32)

    rows = rows_ref[...]
    total = half(rows, in_a, out_a) + half(rows, in_b, out_b)
    result_ref[...] = total.astype(jnp.bfloat16)


def ffn(rows, in_a, in_b, out_a, out_b):
    count, width = rows.shape
    hidden = in_a.shape[2]
    return pl.pallas_call(
        ffn_kernel,
        out_shape=jax.ShapeDtypeStruct((count, width), jnp.bfloat16),
        compiler_params=pltpu.CompilerParams(vmem_limit_bytes=34 * MIB),
        cost_estimate=pl.CostEstimate(
            flops=8 * count * width * hidden, bytes_accessed=8 * width * hidden, transcendentals=0
        ),
        name="ffn",
    )(rows, in_a, in_b, out_a, out_b)


def mix_kernel(experts_ref, slots_ref, gating_ref, tokens_ref, returned_ref, out_ref, *, capacity):
    pick = picks(experts_ref, slots_ref, returned_ref.shape[0], capacity)
    arrived = lax.dot_general(
        pick, returned_ref[...], (((0,), (0,)), ((), ())), preferred_element_type=jnp.float32
    )
    gating = jnp.broadcast_to(gating_ref[...], (8, gating_ref.shape[1])).T[:, :1]
    out_ref[...] = (tokens_ref[...].astype(jnp.float32) + gating * arrived).astype(jnp.bfloat16)


def mix(expert_ids, slot_ids, gating, tokens, returned, capacity):
    return pl.pallas_call(
        functools.partial(mix_kernel, capacity=capacity),
        out_shape=jax.ShapeDtypeStruct(tokens.shape, jnp.bfloat16),
        compiler_params=pltpu.CompilerParams(vmem_limit_bytes=8 * MIB),
        name="mix",
    )(expert_ids[None, :], slot_ids[None, :], gating[None, :], tokens, returned)


def on_device(tokens, expert_ids, slot_ids, centroids, w_in, w_out):
    experts = centroids.shape[0]
    count_rows = tokens.shape[0]
    model_width = tokens.shape[1]
    capacity = 2 * count_rows // experts
    pair = lax.axis_size("grp")
    swap = [(i, (i + 1) % pair) for i in range(pair)]
    far_in = lax.ppermute(w_in, "grp", swap)
    far_out = lax.ppermute(w_out, "grp", swap)
    outgoing = place(expert_ids, slot_ids, tokens, experts * capacity, capacity)
    outgoing = outgoing.reshape(experts, capacity, model_width)
    scores = jnp.dot(tokens, centroids.T, preferred_element_type=jnp.float32)
    columns = jnp.arange(experts, dtype=jnp.int32)
    chosen = jnp.sum(jnp.where(columns[None, :] == expert_ids[:, None], scores, 0.0), axis=1)
    gating = jax.nn.sigmoid(chosen)
    received = lax.all_to_all(outgoing, "ex", split_axis=0, concat_axis=0, tiled=True)
    result = ffn(received.reshape(-1, model_width), w_in, far_in, w_out, far_out)
    returned = lax.all_to_all(
        result.reshape(received.shape), "ex", split_axis=0, concat_axis=0, tiled=True
    )
    return mix(
        expert_ids, slot_ids, gating, tokens, returned.reshape(-1, model_width), capacity
    )


def solution(mesh):
    in_specs = (
        P(("grp", "ex"), None),
        P(("grp", "ex")),
        P(("grp", "ex")),
        P(),
        P("ex", None, "grp"),
        P("ex", "grp", None),
    )
    out_specs = P(("grp", "ex"), None)
    return jax.shard_map(
        on_device, mesh=mesh, in_specs=in_specs, out_specs=out_specs, check_vma=False
    )
```

time: 87.4 us -> 77.4 us (0.89)
  matrix products: 19.2 us -> 0.27 us
  Pallas kernels: 0 us -> 11.5 us
  other arithmetic: 1.73 us -> 0.01 us
  local copies, waits for them, and re-layouts: 3.59 us -> 2.43 us
    dot_general x2 -> x0, matrix products: 18.9 us -> none  [half(): return jnp.dot(hidden, second, preferred_element_type=jnp.float32)]
    pallas_call x0 -> x3, Pallas kernels: none -> 11.5 us  [the longest x1 9.8 us: ffn(): pl.pallas_call(ffn_kernel, out_shape=jax.ShapeDtypeStruct((count, width),...]
    unnamed x6 -> x18, local copies, waits for them, and re-layouts: 0.01 us -> 2.43 us
    scatter x1 -> x0, local copies, waits for them, and re-layouts: 2.41 us -> none  [on_device(): jnp.zeros((experts * capacity, model_width), jnp.bfloat16).at[buffer_rows]]
    gather x1 -> x0, local copies, waits for them, and re-layouts: 1.17 us -> none  [on_device(): arrived = returned.reshape(-1, model_width)[buffer_rows]]
    convert_element_type x1 -> x0, other arithmetic: 1.02 us -> none  [on_device(): return mixed_rows.astype(jnp.bfloat16)]
  transfers between devices with their start and end apart: 3 -> 3, of which waited for: 1 -> 1; matrix products, arithmetic and copies ran while one was open for 15% -> 0% of each run, Pallas kernels for 0% -> 1%
where the time goes in v2:
time: 77.4 us; the launch traced here: 77.1 us
  blocking collectives  33.2 us (43%)
  waiting for transfers between devices  24.5 us (32%)
  Pallas kernels  11.5 us (15%)
  starting transfers between devices  5.07 us (7%)
  local copies, waits for them, and re-layouts  2.43 us (3%)
    all_to_all x1, blocking collectives, on_device(): lax.all_to_all(outgoing, 'ex', split_axis=0, concat_axis=0, tiled=True)  33.2 us
    all_to_all x1, waiting for transfers between devices, on_device(): lax.all_to_all(result.reshape(received.shape), 'ex', split_axis=0, concat...  24.5 us
    pallas_call x1, Pallas kernels, ffn(): pl.pallas_call(ffn_kernel, out_shape=jax.ShapeDtypeStruct((count, width),...  9.8 us
    all_to_all x1, starting transfers between devices, on_device(): lax.all_to_all(result.reshape(received.shape), 'ex', split_axis=0, concat...  4.56 us
    unnamed x18, local copies, waits for them, and re-layouts  2.43 us
  transfers between devices with their start and end apart: 3, of which 1 were waited for; matrix products, arithmetic and copies ran while one was open for 0% of the time, Pallas kernels for 1%

profile of v2, /device:TPU:8, one launch (start us, length us, event | category | flops | bytes accessed | tf_op | source)
XLA Modules:
  0.0 77.1 jit_solution(17734997009402687177)
XLA Ops:
  0.0 0.0 copy-start
  0.0 0.0 collective-permute-start
  0.0 0.5 collective-permute-start.1
  0.5 0.0 copy-start.1
  0.5 1.0 %copy-done.1 = bf16[256,1024]{1,0:T(8,128)(2,1)S(1)} copy-done((bf16[256,1024]{1,0:T(8,128)(2,1)S(1)}, bf16[256,1024]{1,0:T(8,128)(2,1)}, u32[]{:S(2)}) %copy-start.1) | copy-done | bytes 524312
  1.6 0.0 copy-start.3
  1.6 0.7 copy-done.3
  2.2 0.0 copy-start.5
  2.2 0.7 copy-done.5
  2.9 0.0 copy-start.7
  2.9 0.0 copy-start.8
  2.9 0.4 place.1
  3.4 33.2 %all_to_all.10 = bf16[16,32,1024]{2,1,0:T(8,128)(2,1)S(1)} all-to-all(bf16[16,32,1024]{2,1,0:T(8,128)(2,1)S(1)} %bitcast.11), channel_id=1, replica_groups=mesh['grp'=2,'ex'=16] {'ex'}, dimensions={0} | all-to-all | bytes 2097152 | tf_op jit(solution)/shard_map/all_to_all | solution.py:96
  36.6 0.0 collective-permute-done.in_b
  36.6 0.0 collective-permute-done.1.out_b
  36.6 0.0 copy-done.7
  36.6 0.0 copy-done.8
  36.6 0.0 copy-start.2
  36.6 0.0 copy-start.4
  36.6 0.0 copy-start.6
  36.6 9.8 %ffn.1 = bf16[512,1024]{1,0:T(8,128)(2,1)} custom-call(bf16[512,1024]{1,0:T(8,128)(2,1)S(1)} %bitcast.10, bf16[1,1024,2048]{2,1,0:T(8,128)(2,1)S(1)} %copy-done.7, bf16[1,1024,2048]{2,1,0:T(8,128)(2,1)S(1)} %collective-permute-done.in_b, bf16[1,2048,1024]{2,1,0:T(8,128)(2,1)S(1)} %copy-done.8, bf16[1,2048,1024]{2,1,0:T(8,128)(2,1)S(1)} %collective-permute-done.1.out_b), custom_call_target="tpu_custom_call" | custom-call | flops 8589934592 | bytes 16777216 | tf_op jit(solution)/shard_map/ffn/pallas_call | solution.py:52
  46.4 4.6 %all-to-all-start.1 = ((bf16[16,32,1024]{2,1,0:T(8,128)(2,1)}), bf16[16,32,1024]{2,1,0:T(8,128)(2,1)S(1)}, u32[]{:S(2)}, u32[]{:S(2)}) async-start(bf16[16,32,1024]{2,1,0:T(8,128)(2,1)} %bitcast.5), calls=%async_computation.1 | async-start | bytes 2097152 | tf_op jit(solution)/shard_map/all_to_all | solution.py:98
  51.0 0.0 copy-done
  51.0 0.0 copy-done.2
  51.0 0.0 copy-done.4
  51.0 0.3 fusion
  51.3 24.5 %all-to-all-done.1 = bf16[16,32,1024]{2,1,0:T(8,128)(2,1)S(1)} async-done(((bf16[16,32,1024]{2,1,0:T(8,128)(2,1)}), bf16[16,32,1024]{2,1,0:T(8,128)(2,1)S(1)}, u32[]{:S(2)}, u32[]{:S(2)}) %all-to-all-start.1) | async-done | bytes 1048608 | tf_op jit(solution)/shard_map/all_to_all | solution.py:98
  75.8 0.0 copy-done.6
  75.8 1.3 %mix.1 = bf16[256,1024]{1,0:T(8,128)(2,1)} custom-call(s32[1,256]{1,0:T(1,128)S(1)} %bitcast.13, s32[1,256]{1,0:T(1,128)S(1)} %bitcast.16, f32[1,256]{1,0:T(1,128)S(1)} %bitcast.14, bf16[256,1024]{1,0:T(8,128)(2,1)S(1)} %copy-done.2, bf16[512,1024]{1,0:T(8,128)(2,1)S(1)} %bitcast.9), custom_call_target="tpu_custom_call" | custom-call | tf_op jit(solution)/shard_map/mix/pallas_call | solution.py:73
  (1 shorter events, 0.0 us)
Async XLA Ops:
  0.0 51.0 %copy-start = (bf16[16,1024]{1,0:T(8,128)(2,1)S(1)}, bf16[16,1024]{1,0:T(8,128)(2,1)}, u32[]{:S(2)}) copy-start(bf16[16,1024]{1,0:T(8,128)(2,1)} %param.9) | copy-start | bytes 98308
  0.0 36.6 %collective-permute-start = (bf16[1,1024,2048]{2,1,0:T(8,128)(2,1)}, bf16[1,1024,2048]{2,1,0:T(8,128)(2,1)S(1)}, u32[]{:S(2)}, u32[]{:S(2)}) collective-permute-start(bf16[1,1024,2048]{2,1,0:T(8,128)(2,1)} %in_a.1), channel_id=1, source_target_pairs={{0,16},{16,0},{1,17},{17,1},{2,18},{18,2},{3,19},{19,3},{4,20},{20... | collective-permute-start | bytes 12582920 | tf_op jit(solution)/shard_map/ppermute | solution.py:88
  0.0 36.6 %collective-permute-start.1 = (bf16[1,2048,1024]{2,1,0:T(8,128)(2,1)}, bf16[1,2048,1024]{2,1,0:T(8,128)(2,1)S(1)}, u32[]{:S(2)}, u32[]{:S(2)}) collective-permute-start(bf16[1,2048,1024]{2,1,0:T(8,128)(2,1)} %out_a.1), channel_id=1, source_target_pairs={{0,16},{16,0},{1,17},{17,1},{2,18},{18,2},{3,19},{19,3},{4,20},{20... | collective-permute-start | bytes 12582920 | tf_op jit(solution)/shard_map/ppermute | solution.py:89
  0.5 1.0 %copy-start.1 = (bf16[256,1024]{1,0:T(8,128)(2,1)S(1)}, bf16[256,1024]{1,0:T(8,128)(2,1)}, u32[]{:S(2)}) copy-start(bf16[256,1024]{1,0:T(8,128)(2,1)} %tokens_ref.3) | copy-start | bytes 1572868
  1.6 0.7 copy-start.3
  2.2 0.7 copy-start.5
  2.9 33.7 %copy-start.7 = (bf16[1,1024,2048]{2,1,0:T(8,128)(2,1)S(1)}, bf16[1,1024,2048]{2,1,0:T(8,128)(2,1)}, u32[]{:S(2)}) copy-start(bf16[1,1024,2048]{2,1,0:T(8,128)(2,1)} %in_a.1) | copy-start | bytes 12582916
  2.9 33.7 %copy-start.8 = (bf16[1,2048,1024]{2,1,0:T(8,128)(2,1)S(1)}, bf16[1,2048,1024]{2,1,0:T(8,128)(2,1)}, u32[]{:S(2)}) copy-start(bf16[1,2048,1024]{2,1,0:T(8,128)(2,1)} %out_a.1) | copy-start | bytes 12582916
  36.6 14.4 %copy-start.2 = (bf16[256,1024]{1,0:T(8,128)(2,1)S(1)}, bf16[256,1024]{1,0:T(8,128)(2,1)}, u32[]{:S(2)}) copy-start(bf16[256,1024]{1,0:T(8,128)(2,1)} %tokens_ref.3) | copy-start | bytes 1572868
  36.6 14.4 %copy-start.4 = (s32[256]{0:T(256)S(1)}, s32[256]{0:T(256)}, u32[]{:S(2)}) copy-start(s32[256]{0:T(256)} %param.7) | copy-start | bytes 3076
  36.6 39.2 %copy-start.6 = (s32[256]{0:T(256)S(1)}, s32[256]{0:T(256)}, u32[]{:S(2)}) copy-start(s32[256]{0:T(256)} %param.8) | copy-start | bytes 3076
  46.4 29.4 %all-to-all-start.1 = ((bf16[16,32,1024]{2,1,0:T(8,128)(2,1)}), bf16[16,32,1024]{2,1,0:T(8,128)(2,1)S(1)}, u32[]{:S(2)}, u32[]{:S(2)}) async-start(bf16[16,32,1024]{2,1,0:T(8,128)(2,1)} %bitcast.5), calls=%async_computation.1 | async-start | bytes 2097152 | tf_op jit(solution)/shard_map/all_to_all | solution.py:98
